TPU v7x, 32 devices: a whole 2x2x4 slice. The times are simulated.
32 devices in a mesh: cells: 8 (over z, x), genes: 4 (over y, core).
Axes of the slice: x: 2, y: 2, z: 4, core: 2. Of those that a mesh axis runs over, the one named last changes fastest.
Arguments:
- expression: float32 [2048, 8192], P('cells', 'genes'), may hold values from 0.1 to 3000, as said below
- donor_label: int32 [2048], P('cells'), may hold values from 0 to 255
- live_count: int32 [8], P('cells'), may hold values from 16 to 256, as said below
- genotypes: bfloat16 [4, 8, 256, 4096], P('genes', 'cells'), may hold values from 0 to 2
- covariates: float32 [256, 2], replicated, may hold values from -4 to 4
- donor_cells: int32 [256], replicated, may hold values from 200 to 4999
- win_start: int32 [4, 2048], P('genes', 'cells'), may hold values from 0 to 2048
- win_len: int32 [4, 2048], P('genes', 'cells'), may hold values from 512 to 2048, as said below
Outputs:
- correlation: float32 [4, 2048, 4096], P('genes', 'cells')
- zscore_out: float32 [4, 2048, 256], P('genes', 'cells')
Inputs may be any that keep to these rules, and one draw needn't show every extreme that they name: `live_count`: some index of cells has all 256 slots used. win_len[b0, k] is 2048 wherever k is a multiple of 256, so win_start + win_len <= 4096 throughout. `expression`: positive counts.
All inputs are finite; a program needn't handle non-finite values.
Results may differ from a plain program's by a relative error of at most 0.0003.
Values sent between devices are 32-bit elements; how exact they have to be, the bound alone decides.
A program may use at most 64 MiB of HBM per device.

v0:
```python
import jax
import jax.numpy as jnp
from jax import lax
from jax.sharding import PartitionSpec as P

HIGHEST = lax.Precision.HIGHEST
epsilon = 1e-06
cpm_scale = 10000.0


def design_matrix(covariates, donor_cells):
    log_cells = jnp.log(donor_cells.astype(jnp.float32) / 1000.0)
    ones_col = jnp.ones((covariates.shape[0], 1), jnp.float32)
    return jnp.concatenate([ones_col, log_cells[:, None], covariates], axis=1)


def invert(gram_matrix):
    width = gram_matrix.shape[0]
    augmented = jnp.concatenate([gram_matrix, jnp.eye(width, dtype=jnp.float32)], axis=1)
    for pivot in range(width):
        pivot_row = augmented[pivot] / augmented[pivot, pivot]
        augmented = augmented - augmented[:, pivot][:, None] * pivot_row[None, :]
        augmented = augmented.at[pivot].set(pivot_row)
    return augmented[:, width:]


def residualize_rows(level_rows, design, gram_inv):
    projected = jnp.dot(level_rows, design, precision=HIGHEST, preferred_element_type=jnp.float32)
    coeffs = jnp.dot(projected, gram_inv, precision=HIGHEST, preferred_element_type=jnp.float32)
    return level_rows - jnp.dot(
        coeffs, design.T, precision=HIGHEST, preferred_element_type=jnp.float32
    )


def body(
    expression, donor_label, live_count, genotypes, covariates, donor_cells, win_start, win_len
):
    donors = covariates.shape[0]
    capacity, local_genes = expression.shape
    cells_count = lax.axis_size("cells")
    block_genes = local_genes // cells_count
    design = design_matrix(covariates, donor_cells)
    gram_inv = invert(
        jnp.dot(design.T, design, precision=HIGHEST, preferred_element_type=jnp.float32)
    )
    donor_ids = jnp.arange(donors, dtype=jnp.int32)
    block_rows = min(128, capacity)
    block_count = (live_count[0] + block_rows - 1) // block_rows

    def onehot_of(labels, usable):
        return ((labels[None, :] == donor_ids[:, None]) & usable[None, :]).astype(jnp.float32)

    def local_block(turn_id):
        offset = turn_id * block_rows
        cell_rows = lax.dynamic_slice_in_dim(expression, offset, block_rows, 0)
        labels = lax.dynamic_slice_in_dim(donor_label, offset, block_rows, 0)
        usable = offset + jnp.arange(block_rows, dtype=jnp.int32) < live_count[0]
        return (cell_rows, onehot_of(labels, usable))

    def gene_major(turn_id, running):
        cell_rows, onehot = local_block(turn_id)
        return running + lax.dot_general(
            cell_rows,
            onehot,
            (((0,), (1,)), ((), ())),
            precision=HIGHEST,
            preferred_element_type=jnp.float32,
        )

    partial_value = lax.fori_loop(
        0, block_count, gene_major, jnp.zeros((local_genes, donors), jnp.float32)
    )
    totals = lax.psum(jnp.sum(partial_value, axis=0), ("cells", "genes"))
    pieces = lax.all_to_all(partial_value, "cells", split_axis=0, concat_axis=0, tiled=True)
    sums_rows = jnp.sum(pieces.reshape(cells_count, block_genes, donors), axis=0)
    level_rows = jnp.log1p(cpm_scale * sums_rows / (totals[None, :] + 1.0))
    level_rows = residualize_rows(level_rows, design, gram_inv)
    zscore_rows = level_rows * lax.rsqrt(
        jnp.mean(level_rows * level_rows, axis=1, keepdims=True) + epsilon
    )
    dosage = genotypes[0, 0].astype(jnp.float32)
    coef_x = jnp.dot(
        gram_inv,
        jnp.dot(design.T, dosage, precision=HIGHEST, preferred_element_type=jnp.float32),
        precision=HIGHEST,
        preferred_element_type=jnp.float32,
    )
    dosage_res = dosage - jnp.dot(
        design, coef_x, precision=HIGHEST, preferred_element_type=jnp.float32
    )
    dosage_z = dosage_res * lax.rsqrt(
        jnp.mean(dosage_res * dosage_res, axis=0, keepdims=True) + epsilon
    )
    correlation = (
        jnp.dot(zscore_rows, dosage_z, precision=HIGHEST, preferred_element_type=jnp.float32)
        / donors
    )
    variant = jnp.arange(dosage.shape[1], dtype=jnp.int32)
    first = win_start[0]
    inside = (variant[None, :] >= first[:, None]) & (
        variant[None, :] < (first + win_len[0])[:, None]
    )
    correlation = jnp.where(inside, correlation, jnp.float32(0.0))
    return (correlation[None], zscore_rows[None])


def solution(mesh):
    placed = (
        P("cells", "genes"),
        P("cells"),
        P("cells"),
        P("genes", "cells", None, None),
        P(),
        P(),
        P("genes", "cells"),
        P("genes", "cells"),
    )
    return jax.shard_map(
        body,
        mesh=mesh,
        in_specs=placed,
        out_specs=(P("genes", "cells", None), P("genes", "cells", None)),
        check_vma=False,
    )
```

profile of v0, /device:TPU:0, one launch (start us, length us, event | category | flops | bytes accessed | tf_op | source)
XLA Modules:
  0.0 110.4 jit_solution(6040645947162707037)
XLA Ops:
  1.3 1.5 %broadcast_in_dim.16 = f32[2048,256]{1,0:T(8,128)} broadcast(f32[]{:T(128)} %constant.148.clone.1), dimensions={} | broadcast | bytes 2097156 | tf_op jit(solution)/shard_map/broadcast_in_dim | solution.py:71
  2.8 5.7 %while.15 = (s32[]{:T(128)}, f32[2048,256]{1,0:T(8,128)}, s32[]{:T(128)}, f32[256,2048]{1,0:T(8,128)}, s32[256]{0:T(256)}, /*index=5*/s32[1]{0:T(128)}, s32[]{:T(128)}, s32[]{:T(128)}, s32[]{:T(128)}, s32[]{:T(128)}) while((s32[]{:T(128)}, f32[2048,256]{1,0:T(8,128)}, s32[]{:T(128)}, f32[256,2048]{1,0:T(8,128)}, s32[256]{0:T(256)}, ...), condition=%wide.region_1.0_spmd.clone, body=%wide.region_0.0_spmd.clone.sunk | while | flops 805896448 | bytes 5244843 | solution.py:70
  2.8 0.8 dynamic_slice.13
  3.5 0.7 add_compare_fusion.2
  4.2 4.3 %convolution_add_fusion.2 = f32[2048,256]{1,0:T(8,128)} fusion(f32[2048,256]{1,0:T(8,128)} %get-tuple-element.175, f32[256,2048]{1,0:T(8,128)} %get-tuple-element.187, s32[]{:T(128)S(6)} %select_n.20, s32[128]{0:T(128)S(1)} %dynamic_slice.13, pred[128]{0:T(512)(128)(4,1)S(1)} %add_compare_fusion.2), kind=kOutput, calls=%fused_computation.1.clone.1 | convolution fusion | flops 805896192 | bytes 5243524 | tf_op jit(solution)/shard_map/while/body/dot_general | solution.py:62
  8.4 12.1 %all-to-all-start = ((f32[8,256,256]{2,1,0:T(8,128)}), f32[8,256,256]{2,1,0:T(8,128)S(1)}, u32[]{:S(2)}, u32[]{:S(2)}) async-start(f32[8,256,256]{2,1,0:T(8,128)} %bitcast.3), calls=%async_computation | async-start | bytes 4194304 | tf_op jit(solution)/shard_map/all_to_all | solution.py:74
  21.5 0.7 fusion.32
  22.2 0.7 slice_divide_fusion.3
  22.8 1.9 %reduce_sum.37 = f32[256]{0:T(256)S(1)} reduce(f32[2048,256]{1,0:T(8,128)} %get-tuple-element.88, f32[]{:T(128)} %constant.148.clone.1), dimensions={0}, to_apply=%region_3.0 | reduce | flops 524032 | bytes 2098180 | tf_op jit(solution)/shard_map/reduce_sum | solution.py:73
  24.8 0.6 slice.104
  25.6 0.7 fusion.31
  26.2 0.7 slice_divide_fusion.2
  27.0 0.6 slice.107
  27.8 0.7 fusion.30
  28.4 0.7 slice_divide_fusion.1
  29.2 0.6 slice.110
  30.0 0.7 fusion.29
  30.6 0.7 slice_divide_fusion
  31.4 57.6 %psum.7 = f32[256]{0:T(256)S(1)} all-reduce(f32[256]{0:T(256)S(1)} %reduce_sum.37), channel_id=1, replica_groups=mesh['cells'=8,'genes'=4] {'cells','genes'}, use_global_device_ids=true, to_apply=%region_4.5 | all-reduce | flops 256 | bytes 2048 | tf_op jit(solution)/shard_map/psum | solution.py:73
  89.1 2.5 %fusion.12 = f32[4,4096]{1,0:T(4,128)S(1)} fusion(bf16[1,1,256,4096]{3,2,1,0:T(8,128)(2,1)} %param.21, f32[256,2]{0,1:T(2,128)S(1)} %copy-done, f32[256,1]{0,1:T(1,128)S(1)} %bitcast.34, f32[4]{0:T(128)S(1)} %pad.10.clone), kind=kOutput, calls=%fused_computation.18 | convolution fusion | flops 50333696 | bytes 2165776 | tf_op jit(solution)/shard_map/dot_general | solution.py:84
  92.0 6.8 %multiply_reduce_fusion = (f32[4096]{0:T(1024)S(1)}, f32[256,4096]{1,0:T(8,128)}) fusion(f32[4,4096]{1,0:T(4,128)S(1)} %fusion.19, f32[256,2]{0,1:T(2,128)S(1)} %copy-done, f32[256,1]{0,1:T(1,128)S(1)} %bitcast.35, f32[4]{0:T(128)S(1)} %pad.10.clone, bf16[1,1,256,4096]{3,2,1,0:T(8,128)(2,1)} %param.21), kind=kOutput, calls=%fused_computation.14 | convolution fusion | flops 54523904 | bytes 6376464 | tf_op jit(solution)/shard_map/dot_general | solution.py:88
  99.7 0.6 multiply_reduce_fusion.1
  100.3 0.8 copy.13
  101.2 9.3 %fusion.9 = f32[1,256,4096]{2,1,0:T(8,128)} fusion(f32[256,4096]{1,0:T(8,128)} %get-tuple-element.123, f32[4096]{0:T(1024)S(1)} %add_rsqrt_fusion, s32[256]{0:T(256)S(1)} %add.72, s32[256]{0:T(256)S(1)} %bitcast.39, f32[256,256]{0,1:T(8,128)S(1)} %get-tuple-element.125, f32[256]{0:T(256)S(1)} %add_rsqrt_fusion.1), kind=kOutput, calls=%fused_computation.12 | convolution fusion | flops 3227582464 | bytes 8670208 | tf_op jit(solution)/shard_map/dot_general | solution.py:95
  (37 shorter events, 3.3 us)
Async XLA Ops:
  8.4 12.1 %copy-start.3 = (s32[256]{0:T(256)S(1)}, s32[256]{0:T(256)}, u32[]{:S(2)}) copy-start(s32[256]{0:T(256)} %param.23) | copy-start | bytes 3076
  8.4 12.2 %copy-start = (f32[256,2]{0,1:T(2,128)S(1)}, f32[256,2]{0,1:T(2,128)}, u32[]{:S(2)}) copy-start(f32[256,2]{0,1:T(2,128)} %param.22) | copy-start | bytes 6148
  8.4 21.4 %copy-start.1 = (s32[1,256]{1,0:T(1,128)S(1)}, s32[1,256]{1,0:T(1,128)}, u32[]{:S(2)}) copy-start(s32[1,256]{1,0:T(1,128)} %param.24) | copy-start | bytes 3076
  8.4 21.4 %copy-start.2 = (s32[1,256]{1,0:T(1,128)S(1)}, s32[1,256]{1,0:T(1,128)}, u32[]{:S(2)}) copy-start(s32[1,256]{1,0:T(1,128)} %param.25) | copy-start | bytes 3076
  8.4 90.3 %all-to-all-start = ((f32[8,256,256]{2,1,0:T(8,128)}), f32[8,256,256]{2,1,0:T(8,128)S(1)}, u32[]{:S(2)}, u32[]{:S(2)}) async-start(f32[8,256,256]{2,1,0:T(8,128)} %bitcast.3), calls=%async_computation | async-start | bytes 4194304 | tf_op jit(solution)/shard_map/all_to_all | solution.py:74
where the time goes:
time: 111 us; the launch traced here: 110 us
  blocking collectives  57.6 us (52%)
  matrix products  24.6 us (22%)
  starting transfers between devices  12.1 us (11%)
  other arithmetic  8.3 us (7%)
  local copies, waits for them, and re-layouts  6.28 us (6%)
  between operations  1.47 us (1%)
    psum x1, blocking collectives, body(): totals = lax.psum(jnp.sum(partial_value, axis=0), ('cells', 'genes'))  57.6 us
    all_to_all x1, starting transfers between devices, body(): lax.all_to_all(partial_value, 'cells', split_axis=0, concat_axis=0, tiled...  12.1 us
    dot_general x1, matrix products, body(): jnp.dot(zscore_rows, dosage_z, precision=HIGHEST, preferred_element_type=...  9.3 us
    dot_general x1, matrix products, body(): jnp.dot(design, coef_x, precision=HIGHEST, preferred_element_type=jnp.flo...  6.76 us
    dot_general x1, matrix products, gene_major(): lax.dot_general(cell_rows, onehot, (((0,), (1,)), ((), ())), precision=HI...  4.27 us
    div x4, other arithmetic, invert(): pivot_row = augmented[pivot] / augmented[pivot, pivot]  2.61 us
    mul x4, other arithmetic, invert(): augmented = augmented - augmented[:, pivot][:, None] * pivot_row[None, :]  2.6 us
    dot_general x1, matrix products, body(): jnp.dot(design.T, dosage, precision=HIGHEST, preferred_element_type=jnp.f...  2.55 us
  transfers between devices with their start and end apart: 1, of which 0 were waited for; matrix products, arithmetic and copies ran while one was open for 18% of the time, Pallas kernels for 0%

commit v1 on v0

v1 whole, which is shorter than its diff:
```python
import functools

import jax
import jax.numpy as jnp
from jax import lax
from jax.experimental import pallas as pl
from jax.experimental.pallas import tpu as pltpu
from jax.sharding import PartitionSpec as P

MESH = pl.DeviceIdType.MESH
epsilon = 1e-06
cpm_scale = 10000.0
SPLIT = 2


def halves(value):
    high = value.astype(jnp.bfloat16)
    low = (value - high.astype(jnp.float32)).astype(jnp.bfloat16)
    return high, low


def thirds(value):
    high = value.astype(jnp.bfloat16)
    rest = value - high.astype(jnp.float32)
    mid, low = halves(rest)
    return high, mid, low


def mm(left, right):
    return jnp.dot(left, right, preferred_element_type=jnp.float32)


def inverse_entries(rows):
    width = len(rows)
    gram = [[None] * width for _ in range(width)]
    for i in range(width):
        for j in range(i, width):
            gram[i][j] = jnp.sum(rows[i] * rows[j], axis=1, keepdims=True)
            gram[j][i] = gram[i][j]
    one = jnp.ones((1, 1), jnp.float32)
    zero = jnp.zeros((1, 1), jnp.float32)
    table = [gram[i] + [one if i == j else zero for j in range(width)] for i in range(width)]
    for pivot in range(width):
        top = [entry / table[pivot][pivot] for entry in table[pivot]]
        table = [
            top
            if i == pivot
            else [table[i][j] - table[i][pivot] * top[j] for j in range(2 * width)]
            for i in range(width)
        ]
    return [row[width:] for row in table]


def exchange_kernel(
    n_cells, n_genes,
    expr_hbm, label_ref, live_ref, geno_hbm, cov_ref, cells_ref,
    sums_ref, totals_ref, design_ref, scale_ref,
    expr, geno, onehot, part, xrecv, zrecv, tot_mine, tot_cells, tot_sum, tot_genes,
    load_sem, xs, xr, zs, zr, ts, tr, gs, gr,
):
    cap, local_genes = expr.shape
    donors = onehot.shape[1]
    lines = n_cells // 2
    blk = local_genes // n_cells
    piece = blk // SPLIT
    c = lax.axis_index("cells")
    gene_id = lax.axis_index("genes")
    a = c // 2
    b = lax.rem(c, 2)

    load_expr = pltpu.make_async_copy(expr_hbm, expr, load_sem.at[0])
    load_geno = pltpu.make_async_copy(geno_hbm.at[0, 0], geno, load_sem.at[1])
    load_expr.start()
    load_geno.start()

    barrier = pltpu.get_barrier_semaphore()

    def greet_cells(k, carry):
        pl.semaphore_signal(
            barrier, 1, device_id={"cells": lax.rem(c + k, n_cells)}, device_id_type=MESH
        )
        return carry

    lax.fori_loop(1, n_cells, greet_cells, 0)
    for k in range(1, n_genes):
        pl.semaphore_signal(
            barrier, 1, device_id={"genes": lax.rem(gene_id + k, n_genes)}, device_id_type=MESH
        )

    labels = label_ref[...]
    usable = lax.broadcasted_iota(jnp.int32, (1, cap), 1) < live_ref[0, 0]
    picked = jnp.where(usable, labels, -1)
    donor_ids = lax.broadcasted_iota(jnp.int32, (donors, cap), 0)
    spread = jnp.where(donor_ids == picked, 1.0, 0.0).astype(jnp.float32)
    spread = spread.T
    onehot[...] = spread.astype(jnp.bfloat16)

    load_expr.wait()
    per_cell = jnp.sum(expr[...], axis=1, keepdims=True)
    tot_mine[...] = jnp.sum(spread * per_cell, axis=0, keepdims=True)

    pl.semaphore_wait(barrier, n_cells - 1 + n_genes - 1)

    def send_total(k):
        return pltpu.make_async_remote_copy(
            tot_mine, tot_cells.at[k], ts.at[k], tr.at[k],
            device_id={"cells": lax.rem(c + k, n_cells)}, device_id_type=MESH,
        )

    def start_total(k, carry):
        send_total(k).start()
        return carry

    lax.fori_loop(1, n_cells, start_total, 0)

    def order(k):
        right, left = lines - 1 - a, a
        gap = jnp.abs(right - left)
        j = k - gap
        dist = jnp.minimum(right, left) - j // 2
        near = jnp.where(lax.rem(j, 2) == 0, a + dist, a - dist)
        far = jnp.where(right > left, lines - 1 - k, k)
        return jnp.where(k < gap, far, near)

    def multiply(start, width):
        high, low = halves(expr[:, pl.ds(pl.multiple_of(start, 128), width)])
        dims = (((0,), (0,)), ((), ()))
        hot = onehot[...]
        part[pl.ds(pl.multiple_of(start, 8), width), :] = lax.dot_general(
            high, hot, dims, preferred_element_type=jnp.float32
        ) + lax.dot_general(low, hot, dims, preferred_element_type=jnp.float32)

    def x_copy(d, s):
        row = pl.multiple_of((d * 2 + 1 - b) * blk + s * piece, 8)
        return pltpu.make_async_remote_copy(
            part.at[pl.ds(row, piece)], xrecv.at[d * SPLIT + s],
            xs.at[d * SPLIT + s], xr.at[d * SPLIT + s],
            device_id={"cells": a * 2 + 1 - b}, device_id_type=MESH,
        )

    aligned = blk % 128 == 0

    def send_x(k, carry):
        d = order(k)
        if aligned:
            multiply((d * 2 + 1 - b) * blk, blk)
        for s in range(SPLIT):
            x_copy(d, s).start()
        return carry

    if not aligned:
        wide = min(256, local_genes)

        def all_parts(j, carry):
            multiply(j * wide, wide)
            return carry

        lax.fori_loop(0, local_genes // wide, all_parts, 0)
    lax.fori_loop(0, lines, send_x, 0)
    if aligned:

        def own_part(k, carry):
            multiply((order(k) * 2 + b) * blk, blk)
            return carry

        lax.fori_loop(0, lines, own_part, 0)

    rows = [
        jnp.ones((1, donors), jnp.float32),
        jnp.log(cells_ref[...].astype(jnp.float32) / 1000.0),
        cov_ref[0:1, :],
        cov_ref[1:2, :],
    ]
    inverse = inverse_entries(rows)
    width = len(rows)
    solve = []
    for i in range(width):
        term = inverse[i][0] * rows[0]
        for j in range(1, width):
            term = term + inverse[i][j] * rows[j]
        solve.append(term)
    design_ref[...] = jnp.concatenate(rows + solve, axis=0)

    n_steps = lines * SPLIT
    variants = geno.shape[1]
    wide_v = 128
    while variants // wide_v > n_steps:
        wide_v *= 2
    chunks = variants // wide_v

    load_geno.wait()

    def dosage_chunk(t):
        both = design_ref[...]
        columns = both.T
        span = pl.ds(pl.multiple_of(t * wide_v, 128), wide_v)
        block = geno[:, span]
        p1, p2, p3 = thirds(both)
        coef = mm(p1, block) + mm(p2, block) + mm(p3, block)
        rest = block.astype(jnp.float32)
        for i in range(width):
            rest = rest - columns[:, i : i + 1] * coef[width + i : width + i + 1, :]
        scale_ref[:, span] = lax.rsqrt(
            jnp.mean(rest * rest, axis=0, keepdims=True) + epsilon
        ) / donors

    def z_copy(d, s, side, target):
        row = pl.multiple_of((d * 2 + b) * blk + s * piece, 8)
        slot = (side * lines + d) * SPLIT + s
        return pltpu.make_async_remote_copy(
            part.at[pl.ds(row, piece)], zrecv.at[slot],
            zs.at[d * SPLIT + s], zr.at[slot],
            device_id={"cells": target * 2 + b}, device_id_type=MESH,
        )

    def add_z(d, s, side, rows_of):
        z_copy(d, s, side, a).wait_recv()
        part[rows_of, :] = part[rows_of, :] + zrecv[(side * lines + d) * SPLIT + s]

    def send_genes(k):
        return pltpu.make_async_remote_copy(
            tot_sum, tot_genes.at[k], gs.at[k], gr.at[k],
            device_id={"genes": lax.rem(gene_id + k, n_genes)}, device_id_type=MESH,
        )

    def step(t, carry):
        @pl.when(t < chunks)
        def _():
            dosage_chunk(t)

        k, s = t // SPLIT, lax.rem(t, SPLIT)
        d = order(k)
        rows_of = pl.ds(pl.multiple_of((d * 2 + b) * blk + s * piece, 8), piece)
        x_copy(d, s).wait_recv()
        part[rows_of, :] = part[rows_of, :] + xrecv[d * SPLIT + s]

        @pl.when((d >= a) & (a > 0))
        def _():
            add_z(d, s, 0, rows_of)

        @pl.when((d <= a) & (a < lines - 1))
        def _():
            add_z(d, s, 1, rows_of)

        @pl.when(d > a)
        def _():
            z_copy(d, s, 0, a + 1).start()

        @pl.when(d < a)
        def _():
            z_copy(d, s, 1, a - 1).start()

        @pl.when(d == a)
        def _():
            sums_ref[pl.ds(pl.multiple_of(s * piece, 8), piece), :] = part[rows_of, :]

        @pl.when(t == 1)
        def _():
            def gather_total(k, running):
                send_total(k).wait_recv()
                return running + tot_cells[k]

            tot_sum[...] = lax.fori_loop(1, n_cells, gather_total, tot_mine[...])
            for k in range(1, n_genes):
                send_genes(k).start()

        return carry

    lax.fori_loop(0, n_steps, step, 0)

    total = tot_sum[...]
    for k in range(1, n_genes):
        send_genes(k).wait_recv()
        total = total + tot_genes[k]
    totals_ref[...] = total

    for k in range(1, n_genes):
        send_genes(k).wait_send()

    def drain_total(k, carry):
        send_total(k).wait_send()
        return carry

    lax.fori_loop(1, n_cells, drain_total, 0)

    def drain(t, carry):
        d, s = t // SPLIT, lax.rem(t, SPLIT)
        x_copy(d, s).wait_send()

        @pl.when(d != a)
        def _():
            z_copy(d, s, 0, a).wait_send()

        return carry

    lax.fori_loop(0, n_steps, drain, 0)


def correlate_kernel(
    sums_ref, totals_ref, design_ref, scale_ref, geno_ref, first_ref, length_ref,
    corr_ref, zscore_ref, z_high, z_low, low_end, high_end,
):
    blk, donors = sums_ref.shape
    wide = geno_ref.shape[3]
    width = design_ref.shape[0] // 2

    @pl.when(pl.program_id(0) == 0)
    def _():
        rows = [design_ref[i : i + 1, :] for i in range(2 * width)]

        def residual_of(level):
            coefs = [jnp.sum(level * rows[i], axis=1, keepdims=True) for i in range(width)]
            for i in range(width):
                level = level - coefs[i] * rows[width + i]
            return level

        level = jnp.log1p(cpm_scale * sums_ref[...] / (totals_ref[...] + 1.0))
        level = residual_of(level)
        zscore = level * lax.rsqrt(jnp.mean(level * level, axis=1, keepdims=True) + epsilon)
        zscore_ref[0] = zscore
        high, low = halves(residual_of(zscore))
        z_high[...] = high
        z_low[...] = low
        diagonal = lax.broadcasted_iota(jnp.int32, (blk, blk), 0) == lax.broadcasted_iota(
            jnp.int32, (blk, blk), 1
        )

        def column(row):
            held = jnp.where(diagonal, row.astype(jnp.float32), 0.0)
            return jnp.sum(held, axis=1, keepdims=True).astype(jnp.int32)

        first = column(first_ref[...])
        low_end[...] = first
        high_end[...] = first + column(length_ref[...])

    block = geno_ref[0, 0]
    product = (mm(z_high[...], block) + mm(z_low[...], block)) * scale_ref[...]
    variant = pl.program_id(0) * wide + lax.broadcasted_iota(jnp.int32, (1, wide), 1)
    inside = (variant >= low_end[...]) & (variant < high_end[...])
    corr_ref[0] = jnp.where(inside, product, 0.0)


def body(
    expression, donor_label, live_count, genotypes, covariates, donor_cells, win_start, win_len
):
    n_cells = lax.axis_size("cells")
    n_genes = lax.axis_size("genes")
    donors = covariates.shape[0]
    cap, local_genes = expression.shape
    blk = local_genes // n_cells
    variants = genotypes.shape[3]
    lines = n_cells // 2
    piece = blk // SPLIT
    f32, bf16 = jnp.float32, jnp.bfloat16
    vmem = pl.BlockSpec(memory_space=pltpu.VMEM)
    smem = pl.BlockSpec(memory_space=pltpu.SMEM)
    hbm = pl.BlockSpec(memory_space=pl.ANY)
    dma = pltpu.SemaphoreType.DMA
    sums, totals, design, scale = pl.pallas_call(
        functools.partial(exchange_kernel, n_cells, n_genes),
        out_shape=(
            jax.ShapeDtypeStruct((blk, donors), f32),
            jax.ShapeDtypeStruct((1, donors), f32),
            jax.ShapeDtypeStruct((8, donors), f32),
            jax.ShapeDtypeStruct((1, variants), f32),
        ),
        in_specs=[hbm, vmem, smem, hbm, vmem, vmem],
        out_specs=(vmem, vmem, vmem, vmem),
        scratch_shapes=[
            pltpu.VMEM((cap, local_genes), f32),
            pltpu.VMEM((donors, variants), bf16),
            pltpu.VMEM((cap, donors), bf16),
            pltpu.VMEM((local_genes, donors), f32),
            pltpu.VMEM((lines * SPLIT, piece, donors), f32),
            pltpu.VMEM((2 * lines * SPLIT, piece, donors), f32),
            pltpu.VMEM((1, donors), f32),
            pltpu.VMEM((n_cells, 1, donors), f32),
            pltpu.VMEM((1, donors), f32),
            pltpu.VMEM((n_genes, 1, donors), f32),
            dma((2,)),
            dma((lines * SPLIT,)),
            dma((lines * SPLIT,)),
            dma((lines * SPLIT,)),
            dma((2 * lines * SPLIT,)),
            dma((n_cells,)),
            dma((n_cells,)),
            dma((n_genes,)),
            dma((n_genes,)),
        ],
        compiler_params=pltpu.CompilerParams(
            collective_id=0, has_side_effects=True, vmem_limit_bytes=40 << 20
        ),
        name="exchange",
    )(
        expression,
        donor_label.reshape(1, cap),
        live_count.reshape(1, 1),
        genotypes,
        covariates.T,
        donor_cells.reshape(1, donors),
    )
    wide = min(1024, variants)
    whole = lambda shape: pl.BlockSpec(shape, lambda i: (0,) * len(shape))
    correlation, zscore = pl.pallas_call(
        correlate_kernel,
        grid=(variants // wide,),
        out_shape=(
            jax.ShapeDtypeStruct((1, blk, variants), f32),
            jax.ShapeDtypeStruct((1, blk, donors), f32),
        ),
        in_specs=[
            whole((blk, donors)),
            whole((1, donors)),
            whole((8, donors)),
            pl.BlockSpec((1, wide), lambda i: (0, i)),
            pl.BlockSpec((1, 1, donors, wide), lambda i: (0, 0, 0, i)),
            whole((1, blk)),
            whole((1, blk)),
        ],
        out_specs=(
            pl.BlockSpec((1, blk, wide), lambda i: (0, 0, i)),
            whole((1, blk, donors)),
        ),
        scratch_shapes=[
            pltpu.VMEM((blk, donors), bf16),
            pltpu.VMEM((blk, donors), bf16),
            pltpu.VMEM((blk, 1), jnp.int32),
            pltpu.VMEM((blk, 1), jnp.int32),
        ],
        name="correlate",
    )(sums, totals, design, scale, genotypes, win_start, win_len)
    return correlation, zscore


def solution(mesh):
    placed = (
        P("cells", "genes"),
        P("cells"),
        P("cells"),
        P("genes", "cells", None, None),
        P(),
        P(),
        P("genes", "cells"),
        P("genes", "cells"),
    )
    return jax.shard_map(
        body,
        mesh=mesh,
        in_specs=placed,
        out_specs=(P("genes", "cells", None), P("genes", "cells", None)),
        check_vma=False,
    )
```

time: 111 us -> 47.1 us (0.42)
  blocking collectives: 57.6 us -> 0 us
  Pallas kernels: 0 us -> 37.8 us
  matrix products: 24.6 us -> 0 us
  starting transfers between devices: 12.1 us -> 0 us
  other arithmetic: 8.3 us -> 0 us
  local copies, waits for them, and re-layouts: 6.28 us -> 7.68 us
    psum x1 -> x0, blocking collectives: 57.6 us -> none  [body(): totals = lax.psum(jnp.sum(partial_value, axis=0), ('cells', 'genes'))]
    pallas_call x0 -> x2, Pallas kernels: none -> 37.8 us  [the longest x1 32 us: body(): pl.pallas_call(functools.partial(exchange_kernel, n_cells, n_genes), out_...]
    dot_general x9 -> x0, matrix products: 24.6 us -> none  [the longest x1 9.3 us: body(): jnp.dot(zscore_rows, dosage_z, precision=HIGHEST, preferred_element_type=...]
    all_to_all x1 -> x0, starting transfers between devices: 12.1 us -> none  [body(): lax.all_to_all(partial_value, 'cells', split_axis=0, concat_axis=0, tiled...]
    unnamed x9 -> x18, local copies, waits for them, and re-layouts: 0.85 us -> 7.68 us
    slice x8 -> x0, local copies, waits for them, and re-layouts: 2.94 us -> none  [the longest x4 2.28 us: invert(): pivot_row = augmented[pivot] / augmented[pivot, pivot]]
    div x4 -> x0, other arithmetic: 2.61 us -> none  [invert(): pivot_row = augmented[pivot] / augmented[pivot, pivot]]
    mul x4 -> x0, other arithmetic: 2.6 us -> none  [invert(): augmented = augmented - augmented[:, pivot][:, None] * pivot_row[None, :]]
  transfers between devices with their start and end apart: 1 -> 0, of which waited for: 0 -> 0; matrix products, arithmetic and copies ran while one was open for 18% -> 0% of each run, Pallas kernels for 0% -> 0%
where the time goes in v1:
time: 47.1 us; the launch traced here: 46.8 us
  Pallas kernels  37.8 us (80%)
  local copies, waits for them, and re-layouts  7.68 us (16%)
  between operations  1.31 us (3%)
    pallas_call x1, Pallas kernels, body(): pl.pallas_call(functools.partial(exchange_kernel, n_cells, n_genes), out_...  32 us
    unnamed x18, local copies, waits for them, and re-layouts  7.68 us
    pallas_call x1, Pallas kernels, body(): pl.pallas_call(correlate_kernel, grid=(variants // wide,), out_shape=(jax...  5.79 us

profile of v1, /device:TPU:0, one launch (start us, length us, event | category | flops | bytes accessed | tf_op | source)
XLA Modules:
  0.0 46.8 jit_solution(7182688311076071930)
XLA Ops:
  1.3 0.0 copy-start
  1.3 1.6 %copy-done = bf16[1,1,256,4096]{3,2,1,0:T(8,128)(2,1)S(1)} copy-done((bf16[1,1,256,4096]{3,2,1,0:T(8,128)(2,1)S(1)}, bf16[1,1,256,4096]{3,2,1,0:T(8,128)(2,1)}, u32[]{:S(2)}) %copy-start) | copy-done | bytes 2097176
  2.9 0.0 copy-start.1
  2.9 1.6 %copy-done.1 = f32[256,2048]{1,0:T(8,128)S(1)} copy-done((f32[256,2048]{1,0:T(8,128)S(1)}, f32[256,2048]{1,0:T(8,128)}, u32[]{:S(2)}) %copy-start.1) | copy-done | bytes 2097176
  4.5 0.0 copy-start.5
  4.5 0.7 %copy-done.5 = f32[256,2]{0,1:T(2,128)S(1)} copy-done((f32[256,2]{0,1:T(2,128)S(1)}, f32[256,2]{0,1:T(2,128)}, u32[]{:S(2)}) %copy-start.5) | copy-done | bytes 2072
  5.1 0.0 copy-start.7
  5.1 0.7 %copy-done.7 = s32[256]{0:T(256)S(1)} copy-done((s32[256]{0:T(256)S(1)}, s32[256]{0:T(256)}, u32[]{:S(2)}) %copy-start.7) | copy-done | bytes 1048
  5.8 0.0 copy-start.8
  5.8 0.7 %copy-done.8 = s32[256]{0:T(256)S(1)} copy-done((s32[256]{0:T(256)S(1)}, s32[256]{0:T(256)}, u32[]{:S(2)}) %copy-start.8) | copy-done | bytes 1048
  6.5 32.0 %exchange.1 = (f32[256,256]{1,0:T(8,128)S(1)}, f32[1,256]{1,0:T(1,128)S(1)}, f32[8,256]{1,0:T(8,128)S(1)}, f32[1,4096]{1,0:T(1,128)S(1)}) custom-call(f32[256,2048]{1,0:T(8,128)S(1)} %copy-done.1, s32[1,256]{1,0:T(1,128)S(1)} %bitcast.6, s32[1,1]{1,0:T(1,128)} %bitcast.4.live_ref, bf16[1,1,256,4096]{3,2,1,0:T(8,128)(2,1)S(1)} %copy-done, ...), custom_call_target="tpu_custom_call" | custom-call | tf_op jit(solution)/shard_map/exchange/pallas_call | solution.py:359
  38.5 0.0 copy-start.2
  38.5 0.7 %copy-done.2 = f32[256,256]{1,0:T(8,128)} copy-done((f32[256,256]{1,0:T(8,128)}, f32[256,256]{1,0:T(8,128)S(1)}, u32[]{:S(2)}) %copy-start.2) | copy-done | bytes 262168
  39.2 0.0 copy-start.3
  39.2 0.6 %copy-done.3 = f32[1,4096]{1,0:T(1,128)} copy-done((f32[1,4096]{1,0:T(1,128)}, f32[1,4096]{1,0:T(1,128)S(1)}, u32[]{:S(2)}) %copy-start.3) | copy-done | bytes 16408
  39.8 0.0 copy-start.4
  39.8 0.6 %copy-done.4 = f32[8,256]{1,0:T(8,128)} copy-done((f32[8,256]{1,0:T(8,128)}, f32[8,256]{1,0:T(8,128)S(1)}, u32[]{:S(2)}) %copy-start.4) | copy-done | bytes 8216
  40.4 0.0 copy-start.6
  40.4 0.6 %copy-done.6 = f32[1,256]{1,0:T(1,128)} copy-done((f32[1,256]{1,0:T(1,128)}, f32[1,256]{1,0:T(1,128)S(1)}, u32[]{:S(2)}) %copy-start.6) | copy-done | bytes 1048
  41.0 5.8 %correlate.1 = (f32[1,256,4096]{2,1,0:T(8,128)}, f32[1,256,256]{2,1,0:T(8,128)}) custom-call(f32[256,256]{1,0:T(8,128)} %copy-done.2, f32[1,256]{1,0:T(1,128)} %copy-done.6, f32[8,256]{1,0:T(8,128)} %copy-done.4, f32[1,4096]{1,0:T(1,128)} %copy-done.3, bf16[1,1,256,4096]{3,2,1,0:T(8,128)(2,1)} %geno_ref.1, s32[1,256]{1,0:T(1,128)} %first_ref.1, ...), custom_call_target="tpu_custom_call" | custom-call | tf_op jit(solution)/shard_map/correlate/pallas_call | solution.py:404
Async XLA Ops:
  1.3 1.6 %copy-start = (bf16[1,1,256,4096]{3,2,1,0:T(8,128)(2,1)S(1)}, bf16[1,1,256,4096]{3,2,1,0:T(8,128)(2,1)}, u32[]{:S(2)}) copy-start(bf16[1,1,256,4096]{3,2,1,0:T(8,128)(2,1)} %geno_ref.1) | copy-start | bytes 6291460
  2.9 1.6 %copy-start.1 = (f32[256,2048]{1,0:T(8,128)S(1)}, f32[256,2048]{1,0:T(8,128)}, u32[]{:S(2)}) copy-start(f32[256,2048]{1,0:T(8,128)} %expr_hbm.1) | copy-start | bytes 6291460
  4.5 0.7 %copy-start.5 = (f32[256,2]{0,1:T(2,128)S(1)}, f32[256,2]{0,1:T(2,128)}, u32[]{:S(2)}) copy-start(f32[256,2]{0,1:T(2,128)} %param.12) | copy-start | bytes 6148
  5.1 0.7 %copy-start.7 = (s32[256]{0:T(256)S(1)}, s32[256]{0:T(256)}, u32[]{:S(2)}) copy-start(s32[256]{0:T(256)} %param.9) | copy-start | bytes 3076
  5.8 0.7 %copy-start.8 = (s32[256]{0:T(256)S(1)}, s32[256]{0:T(256)}, u32[]{:S(2)}) copy-start(s32[256]{0:T(256)} %param.13) | copy-start | bytes 3076
  38.5 0.7 %copy-start.2 = (f32[256,256]{1,0:T(8,128)}, f32[256,256]{1,0:T(8,128)S(1)}, u32[]{:S(2)}) copy-start(f32[256,256]{1,0:T(8,128)S(1)} %get-tuple-element.6.sums_ref) | copy-start | bytes 786436
  39.2 0.6 %copy-start.3 = (f32[1,4096]{1,0:T(1,128)}, f32[1,4096]{1,0:T(1,128)S(1)}, u32[]{:S(2)}) copy-start(f32[1,4096]{1,0:T(1,128)S(1)} %get-tuple-element.9.scale_ref) | copy-start | bytes 49156
  39.8 0.6 %copy-start.4 = (f32[8,256]{1,0:T(8,128)}, f32[8,256]{1,0:T(8,128)S(1)}, u32[]{:S(2)}) copy-start(f32[8,256]{1,0:T(8,128)S(1)} %get-tuple-element.8.design_ref) | copy-start | bytes 24580
  40.4 0.6 %copy-start.6 = (f32[1,256]{1,0:T(1,128)}, f32[1,256]{1,0:T(1,128)S(1)}, u32[]{:S(2)}) copy-start(f32[1,256]{1,0:T(1,128)S(1)} %get-tuple-element.7.totals_ref) | copy-start | bytes 3076

commit v2 on v1

v2 whole, which is shorter than its diff:
```python
import functools

import jax
import jax.numpy as jnp
from jax import lax
from jax.experimental import pallas as pl
from jax.experimental.pallas import tpu as pltpu
from jax.sharding import PartitionSpec as P

MESH = pl.DeviceIdType.MESH
epsilon = 1e-06
cpm_scale = 10000.0


def halves(value):
    high = value.astype(jnp.bfloat16)
    low = (value - high.astype(jnp.float32)).astype(jnp.bfloat16)
    return high, low


def thirds(value):
    high = value.astype(jnp.bfloat16)
    rest = value - high.astype(jnp.float32)
    mid, low = halves(rest)
    return high, mid, low


def mm(left, right):
    return jnp.dot(left, right, preferred_element_type=jnp.float32)


def inverse_entries(rows):
    width = len(rows)
    gram = [[None] * width for _ in range(width)]
    for i in range(width):
        for j in range(i, width):
            gram[i][j] = jnp.sum(rows[i] * rows[j], axis=1, keepdims=True)
            gram[j][i] = gram[i][j]
    one = jnp.ones((1, 1), jnp.float32)
    zero = jnp.zeros((1, 1), jnp.float32)
    table = [gram[i] + [one if i == j else zero for j in range(width)] for i in range(width)]
    for pivot in range(width):
        top = [entry / table[pivot][pivot] for entry in table[pivot]]
        table = [
            top
            if i == pivot
            else [table[i][j] - table[i][pivot] * top[j] for j in range(2 * width)]
            for i in range(width)
        ]
    return [row[width:] for row in table]


def split_of(blk):
    return max(1, min(4, blk // 16))


def exchange_kernel(
    n_cells, n_genes,
    expr_hbm, label_ref, live_ref, geno_hbm, cov_ref, cells_ref,
    zscore_ref, high_ref, low_ref, scale_ref, geno,
    expr, design, columns, solve3, onehot, part, xrecv, zrecv, tot_mine, tot_cells, tot_sum, tot_genes, tot_all,
    load_sem, xs, xr, zs, zr, ts, tr, gs, gr,
):
    cap, local_genes = expr.shape
    donors = onehot.shape[1]
    lines = n_cells // 2
    blk = local_genes // n_cells
    split = split_of(blk)
    piece = blk // split
    aligned = blk % 128 == 0
    c = lax.axis_index("cells")
    gene_id = lax.axis_index("genes")
    a = c // 2
    b = lax.rem(c, 2)

    def order(k):
        right, left = lines - 1 - a, a
        gap = jnp.abs(right - left)
        j = k - gap
        dist = jnp.minimum(right, left) - j // 2
        near = jnp.where(lax.rem(j, 2) == 0, a + dist, a - dist)
        far = jnp.where(right > left, lines - 1 - k, k)
        return jnp.where(k < gap, far, near)

    load_geno = pltpu.make_async_copy(geno_hbm.at[0, 0], geno, load_sem.at[0])

    def load_expr(k):
        if not aligned:
            return pltpu.make_async_copy(expr_hbm, expr, load_sem.at[1])
        side = 1 - b if k < lines else b
        start = pl.multiple_of((order(k % lines) * 2 + side) * blk, 128)
        span = pl.ds(start, blk)
        return pltpu.make_async_copy(expr_hbm.at[:, span], expr.at[:, span], load_sem.at[1 + k])

    loads = n_cells if aligned else 1
    for k in range(loads):
        load_expr(k).start()

    barrier = pltpu.get_barrier_semaphore()

    def greet_cells(k, carry):
        pl.semaphore_signal(
            barrier, 1, device_id={"cells": lax.rem(c + k, n_cells)}, device_id_type=MESH
        )
        return carry

    lax.fori_loop(1, n_cells, greet_cells, 0)
    for k in range(1, n_genes):
        pl.semaphore_signal(
            barrier, 1, device_id={"genes": lax.rem(gene_id + k, n_genes)}, device_id_type=MESH
        )

    labels = label_ref[...]
    usable = lax.broadcasted_iota(jnp.int32, (1, cap), 1) < live_ref[0, 0]
    picked = jnp.where(usable, labels, -1)
    donor_ids = lax.broadcasted_iota(jnp.int32, (donors, cap), 0)
    spread = jnp.where(donor_ids == picked, 1.0, 0.0).astype(jnp.float32)
    spread = spread.T
    onehot[...] = spread.astype(jnp.bfloat16)

    def send_total(k):
        return pltpu.make_async_remote_copy(
            tot_mine, tot_cells.at[k], ts.at[k], tr.at[k],
            device_id={"cells": lax.rem(c + k, n_cells)}, device_id_type=MESH,
        )

    def start_total(k, carry):
        send_total(k).start()
        return carry

    def multiply(start, width):
        high, low = halves(expr[:, pl.ds(pl.multiple_of(start, 128), width)])
        dims = (((0,), (0,)), ((), ()))
        hot = onehot[...]
        part[pl.ds(pl.multiple_of(start, 8), width), :] = lax.dot_general(
            high, hot, dims, preferred_element_type=jnp.float32
        ) + lax.dot_general(low, hot, dims, preferred_element_type=jnp.float32)

    def x_copy(d, p):
        row = pl.multiple_of((d * 2 + 1 - b) * blk + p * piece, 8)
        return pltpu.make_async_remote_copy(
            part.at[pl.ds(row, piece)], xrecv.at[d * split + p],
            xs.at[d * split + p], xr.at[d * split + p],
            device_id={"cells": a * 2 + 1 - b}, device_id_type=MESH,
        )

    def send_x(k, carry):
        for p in range(split):
            x_copy(order(k), p).start()
        return carry

    def send_totals():
        per_cell = jnp.sum(expr[...], axis=1, keepdims=True)
        tot_mine[...] = jnp.sum(spread * per_cell, axis=0, keepdims=True)
        lax.fori_loop(1, n_cells, start_total, 0)

    def greeted():
        pl.semaphore_wait(barrier, n_cells - 1 + n_genes - 1)

    load_expr(0).wait()
    if aligned:

        def x_part(k, carry):
            multiply((order(k) * 2 + 1 - b) * blk, blk)
            return send_x(k, carry)

        def own_part(k, carry):
            multiply((order(k) * 2 + b) * blk, blk)
            return carry

        multiply((order(0) * 2 + 1 - b) * blk, blk)
        greeted()
        send_x(0, 0)
        for k in range(1, loads):
            load_expr(k).wait()
        load_geno.start()
        send_totals()
        lax.fori_loop(1, lines, x_part, 0)
        lax.fori_loop(0, lines, own_part, 0)
    else:
        wide = min(256, local_genes)

        def all_parts(j, carry):
            multiply(j * wide, wide)
            return carry

        load_geno.start()
        lax.fori_loop(0, local_genes // wide, all_parts, 0)
        greeted()
        send_totals()
        lax.fori_loop(0, lines, send_x, 0)

    rows = [
        jnp.ones((1, donors), jnp.float32),
        jnp.log(cells_ref[...].astype(jnp.float32) / 1000.0),
        cov_ref[0:1, :],
        cov_ref[1:2, :],
    ]
    inverse = inverse_entries(rows)
    width = len(rows)
    solve = []
    for i in range(width):
        term = inverse[i][0] * rows[0]
        for j in range(1, width):
            term = term + inverse[i][j] * rows[j]
        solve.append(term)
    both = jnp.concatenate(rows + solve, axis=0)
    design[...] = both
    columns[...] = both.T
    parts = [value.astype(jnp.float32) for value in thirds(both)]
    solve3[...] = jnp.concatenate(parts, axis=0).astype(jnp.bfloat16)

    n_steps = (lines - 1) * split
    variants = geno.shape[1]
    wide_v = 128
    while variants // wide_v > n_steps:
        wide_v *= 2
    chunks = variants // wide_v

    load_geno.wait()

    def dosage_chunk(t):
        span = pl.ds(pl.multiple_of(t * wide_v, 128), wide_v)
        block = geno[:, span]
        found = mm(solve3[...], block)
        coef = found[0:8] + found[8:16] + found[16:24]
        rest = block.astype(jnp.float32)
        for i in range(width):
            rest = rest - columns[:, i : i + 1] * coef[width + i : width + i + 1, :]
        scale_ref[:, span] = lax.rsqrt(
            jnp.mean(rest * rest, axis=0, keepdims=True) + epsilon
        ) / donors

    def z_copy(d, p, side, target):
        row = pl.multiple_of((d * 2 + b) * blk + p * piece, 8)
        slot = (side * lines + d) * split + p
        return pltpu.make_async_remote_copy(
            part.at[pl.ds(row, piece)], zrecv.at[slot],
            zs.at[d * split + p], zr.at[slot],
            device_id={"cells": target * 2 + b}, device_id_type=MESH,
        )

    def add_z(d, p, side, rows_of):
        z_copy(d, p, side, a).wait_recv()
        part[rows_of, :] = part[rows_of, :] + zrecv[(side * lines + d) * split + p]

    def send_genes(k):
        return pltpu.make_async_remote_copy(
            tot_sum, tot_genes.at[k], gs.at[k], gr.at[k],
            device_id={"genes": lax.rem(gene_id + k, n_genes)}, device_id_type=MESH,
        )

    def arrived(d, p):
        rows_of = pl.ds(pl.multiple_of((d * 2 + b) * blk + p * piece, 8), piece)
        x_copy(d, p).wait_recv()
        part[rows_of, :] = part[rows_of, :] + xrecv[d * split + p]

        @pl.when((d >= a) & (a > 0))
        def _():
            add_z(d, p, 0, rows_of)

        @pl.when((d <= a) & (a < lines - 1))
        def _():
            add_z(d, p, 1, rows_of)

        return rows_of

    def step(t, carry):
        @pl.when(t < chunks)
        def _():
            dosage_chunk(t)

        d, p = order(t // split), lax.rem(t, split)
        arrived(d, p)

        @pl.when(d > a)
        def _():
            z_copy(d, p, 0, a + 1).start()

        @pl.when(d < a)
        def _():
            z_copy(d, p, 1, a - 1).start()

        @pl.when(t == min(split, n_steps - 1))
        def _():
            def gather_total(k, running):
                send_total(k).wait_recv()
                return running + tot_cells[k]

            tot_sum[...] = lax.fori_loop(1, n_cells, gather_total, tot_mine[...])
            for k in range(1, n_genes):
                send_genes(k).start()

        return carry

    lax.fori_loop(0, n_steps, step, 0)

    total = tot_sum[...]
    for k in range(1, n_genes):
        send_genes(k).wait_recv()
        total = total + tot_genes[k]
    tot_all[...] = total

    def residual_of(level):
        coefs = [
            jnp.sum(level * design[i : i + 1, :], axis=1, keepdims=True) for i in range(width)
        ]
        for i in range(width):
            level = level - coefs[i] * design[width + i : width + i + 1, :]
        return level

    def own_piece(p, carry):
        rows_of = arrived(a, p)
        here = pl.ds(pl.multiple_of(p * piece, 16), piece)
        level = jnp.log1p(cpm_scale * part[rows_of, :] / (tot_all[...] + 1.0))
        level = residual_of(level)
        zscore = level * lax.rsqrt(jnp.mean(level * level, axis=1, keepdims=True) + epsilon)
        zscore_ref[here, :] = zscore
        high, low = halves(residual_of(zscore))
        high_ref[here, :] = high
        low_ref[here, :] = low
        return carry

    lax.fori_loop(0, split, own_piece, 0)

    for k in range(1, n_genes):
        send_genes(k).wait_send()

    def drain_total(k, carry):
        send_total(k).wait_send()
        return carry

    lax.fori_loop(1, n_cells, drain_total, 0)

    def drain(t, carry):
        d, p = order(t // split), lax.rem(t, split)
        x_copy(d, p).wait_send()

        @pl.when(t < n_steps)
        def _():
            z_copy(d, p, 0, a).wait_send()

        return carry

    lax.fori_loop(0, lines * split, drain, 0)


def correlate_kernel(
    zscore_in, z_high, z_low, scale_ref, geno_ref, first_ref, length_ref,
    corr_ref, zscore_ref, low_end, high_end,
):
    blk = z_high.shape[0]
    wide = corr_ref.shape[2]
    start = pl.multiple_of(pl.program_id(0) * wide, 128)

    @pl.when(pl.program_id(0) == 0)
    def _():
        zscore_ref[0] = zscore_in[...]
        diagonal = lax.broadcasted_iota(jnp.int32, (blk, blk), 0) == lax.broadcasted_iota(
            jnp.int32, (blk, blk), 1
        )

        def column(row):
            held = jnp.where(diagonal, row.astype(jnp.float32), 0.0)
            return jnp.sum(held, axis=1, keepdims=True).astype(jnp.int32)

        first = column(first_ref[...])
        low_end[...] = first
        high_end[...] = first + column(length_ref[...])

    block = geno_ref[:, pl.ds(start, wide)]
    product = mm(z_high[...], block) + mm(z_low[...], block)
    product = product * scale_ref[:, pl.ds(start, wide)]
    variant = start + lax.broadcasted_iota(jnp.int32, (1, wide), 1)
    inside = (variant >= low_end[...]) & (variant < high_end[...])
    corr_ref[0] = jnp.where(inside, product, 0.0)


def body(
    expression, donor_label, live_count, genotypes, covariates, donor_cells, win_start, win_len
):
    n_cells = lax.axis_size("cells")
    n_genes = lax.axis_size("genes")
    donors = covariates.shape[0]
    cap, local_genes = expression.shape
    blk = local_genes // n_cells
    variants = genotypes.shape[3]
    lines = n_cells // 2
    split = split_of(blk)
    piece = blk // split
    f32, bf16 = jnp.float32, jnp.bfloat16
    vmem = pl.BlockSpec(memory_space=pltpu.VMEM)
    smem = pl.BlockSpec(memory_space=pltpu.SMEM)
    hbm = pl.BlockSpec(memory_space=pltpu.HBM)
    dma = pltpu.SemaphoreType.DMA
    pinned = lambda value: pltpu.with_memory_space_constraint(value, pltpu.HBM)
    held = pl.pallas_call(
        functools.partial(exchange_kernel, n_cells, n_genes),
        out_shape=(
            pltpu.VMEM((blk, donors), f32),
            pltpu.VMEM((blk, donors), bf16),
            pltpu.VMEM((blk, donors), bf16),
            pltpu.VMEM((1, variants), f32),
            pltpu.VMEM((donors, variants), bf16),
        ),
        in_specs=[hbm, vmem, smem, hbm, vmem, vmem],
        out_specs=(vmem, vmem, vmem, vmem, vmem),
        scratch_shapes=[
            pltpu.VMEM((cap, local_genes), f32),
            pltpu.VMEM((8, donors), f32),
            pltpu.VMEM((donors, 8), f32),
            pltpu.VMEM((24, donors), bf16),
            pltpu.VMEM((cap, donors), bf16),
            pltpu.VMEM((local_genes, donors), f32),
            pltpu.VMEM((lines * split, piece, donors), f32),
            pltpu.VMEM((2 * lines * split, piece, donors), f32),
            pltpu.VMEM((1, donors), f32),
            pltpu.VMEM((n_cells, 1, donors), f32),
            pltpu.VMEM((1, donors), f32),
            pltpu.VMEM((n_genes, 1, donors), f32),
            pltpu.VMEM((1, donors), f32),
            dma((1 + n_cells,)),
            dma((lines * split,)),
            dma((lines * split,)),
            dma((lines * split,)),
            dma((2 * lines * split,)),
            dma((n_cells,)),
            dma((n_cells,)),
            dma((n_genes,)),
            dma((n_genes,)),
        ],
        compiler_params=pltpu.CompilerParams(
            collective_id=0, has_side_effects=True, vmem_limit_bytes=40 << 20
        ),
        name="exchange",
    )(
        pinned(expression),
        pinned(donor_label.reshape(1, cap)),
        live_count.reshape(1, 1),
        pinned(genotypes),
        pinned(covariates.T),
        pinned(donor_cells.reshape(1, donors)),
    )
    wide = min(1024, variants)
    whole = lambda shape: pl.BlockSpec(shape, lambda i: (0,) * len(shape))
    correlation, zscore = pl.pallas_call(
        correlate_kernel,
        grid=(variants // wide,),
        out_shape=(
            jax.ShapeDtypeStruct((1, blk, variants), f32),
            jax.ShapeDtypeStruct((1, blk, donors), f32),
        ),
        in_specs=[
            vmem,
            vmem,
            vmem,
            vmem,
            vmem,
            whole((1, blk)),
            whole((1, blk)),
        ],
        out_specs=(
            pl.BlockSpec((1, blk, wide), lambda i: (0, 0, i)),
            whole((1, blk, donors)),
        ),
        scratch_shapes=[
            pltpu.VMEM((blk, 1), jnp.int32),
            pltpu.VMEM((blk, 1), jnp.int32),
        ],
        compiler_params=pltpu.CompilerParams(vmem_limit_bytes=40 << 20),
        name="correlate",
    )(*held, win_start, win_len)
    return correlation, zscore


def solution(mesh):
    placed = (
        P("cells", "genes"),
        P("cells"),
        P("cells"),
        P("genes", "cells", None, None),
        P(),
        P(),
        P("genes", "cells"),
        P("genes", "cells"),
    )
    return jax.shard_map(
        body,
        mesh=mesh,
        in_specs=placed,
        out_specs=(P("genes", "cells", None), P("genes", "cells", None)),
        check_vma=False,
    )
```

time: 47.1 us -> 37.1 us (0.79)
  local copies, waits for them, and re-layouts: 7.68 us -> 0.01 us
  Pallas kernels: 37.8 us -> 35.6 us
    unnamed x18 -> x4, local copies, waits for them, and re-layouts: 7.68 us -> 0.01 us
    pallas_call x1, Pallas kernels: 5.79 us -> 3.56 us  [body(): pl.pallas_call(correlate_kernel, grid=(variants // wide,), out_shape=(jax...]
where the time goes in v2:
time: 37.1 us; the launch traced here: 36.9 us
  Pallas kernels  35.6 us (96%)
  between operations  1.32 us (4%)
    pallas_call x1, Pallas kernels, body(): pl.pallas_call(functools.partial(exchange_kernel, n_cells, n_genes), out_...  32.1 us
    pallas_call x1, Pallas kernels, body(): pl.pallas_call(correlate_kernel, grid=(variants // wide,), out_shape=(jax...  3.56 us

profile of v2, /device:TPU:0, one launch (start us, length us, event | category | flops | bytes accessed | tf_op | source)
XLA Modules:
  0.0 36.9 jit_solution(13844162751411663564)
XLA Ops:
  1.3 0.0 copy-start
  1.3 0.0 copy-start.1
  1.3 32.1 %exchange.1 = (f32[256,256]{1,0:T(8,128)S(1)}, bf16[256,256]{1,0:T(8,128)(2,1)S(1)}, bf16[256,256]{1,0:T(8,128)(2,1)S(1)}, f32[1,4096]{1,0:T(1,128)S(1)}, bf16[256,4096]{1,0:T(8,128)(2,1)S(1)}) custom-call(f32[256,2048]{1,0:T(8,128)} %expr_hbm.1, s32[1,256]{1,0:T(1,128)} %bitcast.6, s32[1,1]{1,0:T(1,128)} %bitcast.4.live_ref, ...), custom_call_target="tpu_custom_call" | custom-call | tf_op jit(solution)/shard_map/exchange/pallas_call | solution.py:397
  33.4 0.0 copy-done
  33.4 0.0 copy-done.1
  33.4 3.6 %correlate.1 = (f32[1,256,4096]{2,1,0:T(8,128)}, f32[1,256,256]{2,1,0:T(8,128)}) custom-call(f32[256,256]{1,0:T(8,128)S(1)} %get-tuple-element.7.zscore_in, bf16[256,256]{1,0:T(8,128)(2,1)S(1)} %get-tuple-element.8.z_high, bf16[256,256]{1,0:T(8,128)(2,1)S(1)} %get-tuple-element.9.z_low, f32[1,4096]{1,0:T(1,128)S(1)} %get-tuple-element.10.scale_ref, ...), custom_call_target="tpu_custom_call" | custom-call | tf_op jit(solution)/shard_map/correlate/pallas_call | solution.py:446
Async XLA Ops:
  1.3 32.1 %copy-start = (s32[1,256]{1,0:T(1,128)S(1)}, s32[1,256]{1,0:T(1,128)}, u32[]{:S(2)}) copy-start(s32[1,256]{1,0:T(1,128)} %first_ref.1) | copy-start | bytes 3076
  1.3 32.1 %copy-start.1 = (s32[1,256]{1,0:T(1,128)S(1)}, s32[1,256]{1,0:T(1,128)}, u32[]{:S(2)}) copy-start(s32[1,256]{1,0:T(1,128)} %length_ref.1) | copy-start | bytes 3076

commit v3 on v2

--- a/solution.py
+++ b/solution.py
@@ -441,7 +441,7 @@
         pinned(covariates.T),
         pinned(donor_cells.reshape(1, donors)),
     )
-    wide = min(1024, variants)
+    wide = min(512, variants)
     whole = lambda shape: pl.BlockSpec(shape, lambda i: (0,) * len(shape))
     correlation, zscore = pl.pallas_call(
         correlate_kernel,

time: 37.1 us -> 38.5 us (1.038)
  Pallas kernels: 35.6 us -> 37 us
    pallas_call x1, Pallas kernels: 3.56 us -> 4.99 us  [body(): pl.pallas_call(correlate_kernel, grid=(variants // wide,), out_shape=(jax...]
where the time goes in v3:
time: 38.5 us; the launch traced here: 38.4 us
  Pallas kernels  37 us (96%)
  between operations  1.32 us (3%)
    pallas_call x1, Pallas kernels, body(): pl.pallas_call(functools.partial(exchange_kernel, n_cells, n_genes), out_...  32.1 us
    pallas_call x1, Pallas kernels, body(): pl.pallas_call(correlate_kernel, grid=(variants // wide,), out_shape=(jax...  4.99 us

profile of v3, /device:TPU:0, one launch (start us, length us, event | category | flops | bytes accessed | tf_op | source)
XLA Modules:
  0.0 38.4 jit_solution(8459200068290329033)
XLA Ops:
  1.3 0.0 copy-start
  1.3 0.0 copy-start.1
  1.3 32.1 %exchange.1 = (f32[256,256]{1,0:T(8,128)S(1)}, bf16[256,256]{1,0:T(8,128)(2,1)S(1)}, bf16[256,256]{1,0:T(8,128)(2,1)S(1)}, f32[1,4096]{1,0:T(1,128)S(1)}, bf16[256,4096]{1,0:T(8,128)(2,1)S(1)}) custom-call(f32[256,2048]{1,0:T(8,128)} %expr_hbm.1, s32[1,256]{1,0:T(1,128)} %bitcast.6, s32[1,1]{1,0:T(1,128)} %bitcast.4.live_ref, ...), custom_call_target="tpu_custom_call" | custom-call | tf_op jit(solution)/shard_map/exchange/pallas_call | solution.py:397
  33.4 0.0 copy-done
  33.4 0.0 copy-done.1
  33.4 5.0 %correlate.1 = (f32[1,256,4096]{2,1,0:T(8,128)}, f32[1,256,256]{2,1,0:T(8,128)}) custom-call(f32[256,256]{1,0:T(8,128)S(1)} %get-tuple-element.7.zscore_in, bf16[256,256]{1,0:T(8,128)(2,1)S(1)} %get-tuple-element.8.z_high, bf16[256,256]{1,0:T(8,128)(2,1)S(1)} %get-tuple-element.9.z_low, f32[1,4096]{1,0:T(1,128)S(1)} %get-tuple-element.10.scale_ref, ...), custom_call_target="tpu_custom_call" | custom-call | tf_op jit(solution)/shard_map/correlate/pallas_call | solution.py:446
Async XLA Ops:
  1.3 32.1 %copy-start = (s32[1,256]{1,0:T(1,128)S(1)}, s32[1,256]{1,0:T(1,128)}, u32[]{:S(2)}) copy-start(s32[1,256]{1,0:T(1,128)} %first_ref.1) | copy-start | bytes 3076
  1.3 32.1 %copy-start.1 = (s32[1,256]{1,0:T(1,128)S(1)}, s32[1,256]{1,0:T(1,128)}, u32[]{:S(2)}) copy-start(s32[1,256]{1,0:T(1,128)} %length_ref.1) | copy-start | bytes 3076
